TPU v7x, 32 devices: a 4x4x1 block of a 4x4x8 slice. The times are simulated.
32 devices in a mesh: dp: 1 (over z), tp: 32 (over x, y, core).
Axes of the slice: x: 4, y: 4, z: 1, core: 2. Of those that a mesh axis runs over, the one named last changes fastest.
The devices are a block of a 4x4x8 slice.
Arguments:
- x: bfloat16 [8192, 4096], P(('dp', 'tp'))
- dy: bfloat16 [8192, 4096], P(('dp', 'tp'))
- gate: bfloat16 [8192, 16384], P('dp', 'tp')
- up: bfloat16 [8192, 16384], P('dp', 'tp')
- w_gate: bfloat16 [4096, 16384], P(None, 'tp')
- w_up: bfloat16 [4096, 16384], P(None, 'tp')
- w_down: bfloat16 [16384, 4096], P('tp')
Outputs:
- output 1: bfloat16 [8192, 4096], P(('dp', 'tp'))
- output 2: bfloat16 [4096, 16384], P('dp', 'tp')
- output 3: bfloat16 [4096, 16384], P('dp', 'tp')
- output 4: bfloat16 [16384, 4096], P(('dp', 'tp'))
All inputs are finite; a program needn't handle non-finite values.
Results may differ from a plain program's by a relative error of at most 0.012.
Values are sent between devices in bfloat16 or wider.
A program may use at most 768 MiB of HBM per device.

v0:
```python
import jax
import jax.numpy as jnp


def act(gate, up):
    return jax.nn.silu(gate) * up


def solution(mesh):
    def step(x, dy, gate, up, w_gate, w_up, w_down):
        hidden, back = jax.vjp(act, gate.astype(jnp.float32), up.astype(jnp.float32))
        d_hidden = jnp.dot(dy, w_down.T, preferred_element_type=jnp.float32)
        d_gate, d_up = (g.astype(jnp.bfloat16) for g in back(d_hidden))
        dx = jnp.dot(d_gate, w_gate.T) + jnp.dot(d_up, w_up.T)
        groups = mesh.shape["dp"]

        def by_group(a, b):
            a, b = (t.reshape(groups, -1, t.shape[-1]) for t in (a, b))
            product = jnp.einsum("gta,gtb->gab", a, b, preferred_element_type=jnp.float32)
            return product.astype(jnp.bfloat16).reshape(-1, b.shape[-1])

        return dx, by_group(x, d_gate), by_group(x, d_up), by_group(hidden.astype(jnp.bfloat16), dy)

    return step
```

profile of v0, /device:TPU:97, one launch (start us, length us, event | category | flops | bytes accessed | tf_op | source)
XLA Modules:
  0.0 701.3 jit_solution(15662565077854785459)
XLA Ops:
  7.2 0.1 all-gather.7.cloned.1.call-start
  7.2 0.7 all-gather.7.cloned.1.call-update
  8.0 0.1 all-gather.9.cloned.1.call-start
  8.0 0.7 all-gather.9.cloned.1.call-update
  8.8 0.1 reduce-scatter.5.cloned.1.call-start
  8.9 201.4 %all-gather.7.cloned.1.call-done = bf16[8192,4096]{1,0:T(8,128)(2,1)} async-done(((bf16[256,4096]{1,0:T(8,128)(2,1)}), bf16[8192,4096]{1,0:T(8,128)(2,1)}) %all-gather.7.cloned.1.call-update) | async-done | bytes 67108880 | tf_op args[1]
  210.2 51.2 %fusion.6 = (bf16[8192,512]{1,0:T(8,128)(2,1)}, f32[8192,512]{1,0:T(8,128)}) fusion(bf16[8192,512]{1,0:T(8,128)(2,1)} %param.3, bf16[8192,512]{1,0:T(8,128)(2,1)} %param.2, bf16[8192,4096]{1,0:T(8,128)(2,1)} %all-gather.7.cloned.1.call-done, bf16[512,4096]{1,0:T(8,128)(2,1)} %param.1), kind=kOutput, calls=%fused_computation.13 | convolution fusion | flops 34414264320 | bytes 113246208 | tf_op jit(solution)/dot_general | solution.py:12
  261.5 43.2 %fusion.15 = bf16[8192,4096]{1,0:T(8,128)(2,1)} fusion(bf16[8192,512]{1,0:T(8,128)(2,1)} %get-tuple-element.4, bf16[4096,512]{1,0:T(8,128)(2,1)} %param.4), kind=kOutput, calls=%fused_computation.22 | convolution fusion | flops 34359738368 | bytes 79691776 | tf_op jit(solution)/dot_general | solution.py:14
  304.7 64.4 %convolution_add_fusion = bf16[8192,4096]{1,0:T(8,128)(2,1)} fusion(bf16[8192,4096]{1,0:T(8,128)(2,1)} %fusion.15, bf16[4096,512]{1,0:T(8,128)(2,1)} %param.5, f32[8192,512]{1,0:T(8,128)} %get-tuple-element.5, bf16[8192,512]{1,0:T(8,128)(2,1)} %param.3), kind=kOutput, calls=%fused_computation | convolution fusion | flops 34422652928 | bytes 163577856 | tf_op jit(solution)/dot_general | solution.py:14
  369.1 0.1 reduce-scatter.5.cloned.1.call-update
  369.1 38.0 %all-gather.9.cloned.1.call-done = bf16[8192,4096]{1,0:T(8,128)(2,1)} async-done(((bf16[256,4096]{1,0:T(8,128)(2,1)}), bf16[8192,4096]{1,0:T(8,128)(2,1)}) %all-gather.9.cloned.1.call-update) | async-done | bytes 67108880 | tf_op args[0]
  407.2 49.2 %fusion.13 = bf16[4096,512]{0,1:T(8,128)(2,1)} fusion(bf16[8192,4096]{1,0:T(8,128)(2,1)} %all-gather.9.cloned.1.call-done, f32[8192,512]{1,0:T(8,128)} %get-tuple-element.5, bf16[8192,512]{1,0:T(8,128)(2,1)} %param.3), kind=kOutput, calls=%fused_computation.20 | convolution fusion | flops 34391195648 | bytes 96468992 | tf_op jit(solution)/gta,gtb->gab/dot_general | solution.py:19
  456.4 6.4 copy.1
  462.8 44.6 %fusion.12 = bf16[4096,512]{0,1:T(8,128)(2,1)} fusion(bf16[8192,512]{1,0:T(8,128)(2,1)} %get-tuple-element.4, bf16[8192,4096]{1,0:T(8,128)(2,1)} %all-gather.9.cloned.1.call-done), kind=kOutput, calls=%fused_computation.19 | convolution fusion | flops 34361835520 | bytes 79691776 | tf_op jit(solution)/gta,gtb->gab/dot_general | solution.py:19
  507.4 6.4 copy
  513.8 48.3 %fusion.9 = bf16[512,4096]{1,0:T(8,128)(2,1)} fusion(bf16[8192,4096]{1,0:T(8,128)(2,1)} %all-gather.7.cloned.1.call-done, bf16[8192,512]{1,0:T(8,128)(2,1)} %param.2, bf16[8192,512]{1,0:T(8,128)(2,1)} %param.3), kind=kOutput, calls=%fused_computation.16 | convolution fusion | flops 34395389952 | bytes 88080384 | tf_op jit(solution)/gta,gtb->gab/dot_general | solution.py:19
  562.1 132.5 %reduce-scatter.5.cloned.1.call-done = bf16[256,4096]{1,0:T(8,128)(2,1)} async-done(((bf16[8192,4096]{1,0:T(8,128)(2,1)}), bf16[256,4096]{1,0:T(8,128)(2,1)}) %reduce-scatter.5.cloned.1.call-update) | async-done | bytes 2097168
Async XLA Ops:
  7.2 203.1 %all-gather.7.cloned.1.call-start = ((), (), s32[]{:S(2)}) async-start(), calls=%async_computation.1 | async-start | bytes 69206016 | tf_op args[1]
  8.0 399.2 %all-gather.9.cloned.1.call-start = ((), (), s32[]{:S(2)}) async-start(), calls=%async_computation.2 | async-start | bytes 69206016 | tf_op args[0]
  8.8 685.8 %reduce-scatter.5.cloned.1.call-start = ((), (), s32[]{:S(2)}) async-start(), calls=%async_computation.3 | async-start | bytes 69206016
Sparse Core Ops, SparseCore 0:
  10.1 200.1 all-gather.6
  212.3 194.8 all-gather.8
  411.6 282.8 reduce-scatter.4
where the time goes:
time: 708 us; the launch traced here: 701 us
  waiting for transfers between devices  373 us (53%)
  matrix products  301 us (43%)
  between operations  14 us (2%)
  local copies, waits for them, and re-layouts  12.8 us (2%)
    unnamed x6, waiting for transfers between devices  373 us
    dot_general x3, matrix products, by_group(): jnp.einsum('gta,gtb->gab', a, b, preferred_element_type=jnp.float32)  142 us
    dot_general x2, matrix products, step(): dx = jnp.dot(d_gate, w_gate.T) + jnp.dot(d_up, w_up.T)  108 us
    dot_general x1, matrix products, step(): d_hidden = jnp.dot(dy, w_down.T, preferred_element_type=jnp.float32)  51.2 us
  transfers between devices with their start and end apart: 3, of which 3 were waited for; matrix products, arithmetic and copies ran while one was open for 45% of the time, Pallas kernels for 0%

commit v1 on v0

v1 whole, which is shorter than its diff:
```python
import functools
import math

import jax
import jax.numpy as jnp
from jax import lax
from jax.experimental import pallas as pl
from jax.experimental.pallas import tpu as pltpu
from jax.sharding import PartitionSpec as P

MESH = pl.DeviceIdType.MESH
F32 = jnp.float32
BF16 = jnp.bfloat16
T_RHS = (((1,), (1,)), ((), ()))


def dot(a, b):
    return jnp.dot(a, b, preferred_element_type=F32)


def dot_t(a, b):
    return lax.dot_general(a, b, T_RHS, preferred_element_type=F32)


def kernel(
    side, tile,
    x_in, dy_in, gate, up, w_gate, w_up, w_down,
    dx_out, dwg_out, dwu_out, dwd_out, xg, dyg, sums, partner_sums,
    wg, wu, wd, acc_g, acc_u, acc_d, dyb, xb, gb, ub, dg, du, hid_t, dg_t, du_t, dg0, du0, to_partner, to_ring,
    load, loadw, loadx,
    dy_s, dy_r, dy_ps, dy_pr, x_s, x_r, x_ps, x_pr, rs_s, rs_r, ps_s, ps_r,
):
    n = side * side
    rows, depth = x_in.shape
    half = rows // 2
    ff = gate.shape[1]
    tiles = depth // tile

    me = lax.axis_index("tp")
    core = lax.rem(me, 2)
    chip = lax.div(me, 2)
    cx, cy = lax.div(chip, side), lax.rem(chip, side)
    diagonal = lax.rem(cx + cy, side)

    def device(c, q):
        major = lax.div(q, side)
        minor = lax.rem(lax.rem(q, side) - major + side, side)
        x = major + c * (minor - major)
        y = minor + c * (major - minor)
        return (x * side + y) * 2 + c

    other = 1 - core
    place = (cx + core * (cy - cx)) * side + diagonal
    other_place = (cx + other * (cy - cx)) * side + diagonal
    right = device(core, lax.rem(place + 1, n))
    left = device(core, lax.rem(place + n - 1, n))
    partner = me + 1 - 2 * core
    onward = (right, left)

    def piece(s, i):
        c, at = (core, place) if i < 2 else (other, other_place)
        q = lax.rem(at + n - s, n) if i % 2 == 0 else lax.rem(at + s, n)
        return pl.multiple_of(device(c, q) * rows + (i % 2) * half, half)

    def remote(src, dst, send, recv, to):
        return pltpu.make_async_remote_copy(
            src_ref=src, dst_ref=dst, send_sem=send, recv_sem=recv, device_id={"tp": to}, device_id_type=MESH
        )

    def columns(j):
        return pl.ds(pl.multiple_of(j * tile, tile), tile)

    def forward(src, whole, s, d, sems):
        at = whole.at[pl.ds(piece(s, d), half)]
        return remote(src, at, sems[0].at[d, s], sems[1].at[d, s + 1], onward[d])

    def across(src, whole, s, d, sems):
        at = whole.at[pl.ds(piece(s, d), half)]
        return remote(src, at, sems[2].at[d, s], sems[3].at[d, s], partner)

    def arrived(whole, s, d, sems):
        at = whole.at[pl.ds(piece(s, d), half)]
        return remote(at, at, sems[0].at[d, s], sems[1].at[d, s], onward[d])

    def arrived_across(whole, s, d, sems):
        at = whole.at[pl.ds(piece(s, 2 + d), half)]
        return remote(at, at, sems[2].at[d, s], sems[3].at[d, s], partner)

    def chunk_load(src, buf, i, sem):
        return pltpu.make_async_copy(src, buf.at[pl.ds(i * half, half)], sem.at[i])

    def gather_step(mine, whole, buf, s, sems, sem):
        for d in range(2):

            @pl.when(s == 0)
            def _():
                src = mine.at[pl.ds(d * half, half)]
                forward(src, whole, s, d, sems).start()
                across(src, whole, s, d, sems).start()
                chunk_load(src, buf, d, sem).start()

            @pl.when(s > 0)
            def _():
                arrived(whole, s, d, sems).wait_recv()
                src = whole.at[pl.ds(piece(s, d), half)]

                @pl.when(s < n - 1)
                def _():
                    forward(src, whole, s, d, sems).start()

                across(src, whole, s, d, sems).start()
                chunk_load(src, buf, d, sem).start()

    def gather_rest(whole, buf, s, sems, sem):
        for d in range(2):
            arrived_across(whole, s, d, sems).wait_recv()
            chunk_load(whole.at[pl.ds(piece(s, 2 + d), half)], buf, 2 + d, sem).start()
        for i in range(4):
            chunk_load(whole.at[pl.ds(piece(s, i), half)], buf, i, sem).wait()

    dy_sems = (dy_s, dy_r, dy_ps, dy_pr)
    x_sems = (x_s, x_r, x_ps, x_pr)

    def across_sum(s):
        return remote(to_partner, partner_sums.at[s], ps_s.at[s], ps_r.at[s], partner)

    def ring_sum(s, d):
        src = to_ring.at[pl.ds(d * half, half)]
        return remote(src, sums.at[s, d], rs_s.at[d, s], rs_r.at[d, s], onward[d])

    def term(a_gate, a_up, cols):
        return dot_t(a_gate, wg[cols, :]) + dot_t(a_up, wu[cols, :])

    def weight_loads():
        return [pltpu.make_async_copy(src, dst, loadw.at[i]) for i, (src, dst) in enumerate(((w_down, wd), (w_gate, wg), (w_up, wu)))]

    barrier = pltpu.get_barrier_semaphore()
    for peer in (left, right, partner):
        pl.semaphore_signal(barrier, inc=1, device_id={"tp": peer}, device_id_type=MESH)
    pl.semaphore_wait(barrier, 3)

    def step(s, carry):
        kept = []
        for i in range(4):
            at = pl.ds(piece(s, i), half)
            kept.append(pltpu.make_async_copy(gate.at[at], gb.at[pl.ds(i * half, half)], load.at[4 + i]))
            kept.append(pltpu.make_async_copy(up.at[at], ub.at[pl.ds(i * half, half)], load.at[8 + i]))
        gather_step(dy_in, dyg, dyb, s, dy_sems, load)
        for copy in kept:
            copy.start()

        @pl.when(s == 0)
        def _():
            for copy in weight_loads():
                copy.start()

            def clear(j, carry):
                zero = jnp.zeros((ff, tile), F32)
                for acc in (acc_g, acc_u, acc_d):
                    acc[:, columns(j)] = zero
                return carry

            gather_step(x_in, xg, xb, s, x_sems, loadx)
            lax.fori_loop(0, tiles, clear, 0)
            for copy in weight_loads():
                copy.wait()

        gather_rest(dyg, dyb, s, dy_sems, load)
        for copy in kept:
            copy.wait()

        ff_tile = min(256, ff)

        def activate(j, carry):
            cols = pl.ds(pl.multiple_of(j * ff_tile, ff_tile), ff_tile)
            d_hidden = dot_t(dyb[...], wd[cols, :])
            g, u = gb[:, cols].astype(F32), ub[:, cols].astype(F32)
            sig = jax.nn.sigmoid(g)
            silu = g * sig
            hid_t[cols, :] = (silu * u).astype(BF16).T
            d_up = (d_hidden * silu).astype(BF16)
            d_gate = ((d_hidden * u) * (sig * (1.0 + g * (1.0 - sig)))).astype(BF16)
            du[:, cols] = d_up
            dg[:, cols] = d_gate
            du_t[cols, :] = d_up.T
            dg_t[cols, :] = d_gate.T
            return carry

        lax.fori_loop(0, ff // ff_tile, activate, 0)

        @pl.when(s > 0)
        def _():
            across_sum(s - 1).wait_send()

        def for_partner(j, carry):
            cols = columns(j)
            to_partner[:, cols] = term(dg[rows:, :], du[rows:, :], cols).astype(BF16)
            return carry

        lax.fori_loop(0, tiles, for_partner, 0)
        across_sum(s).start()

        @pl.when(s > 0)
        def _():
            gather_step(x_in, xg, xb, s, x_sems, loadx)

        def down(j, carry):
            cols = columns(j)
            acc_d[:, cols] += dot(hid_t[...], dyb[:, cols])
            return carry

        lax.fori_loop(0, tiles, down, 0)

        @pl.when(s == 0)
        def _():
            dg0[...] = dg[:rows, :]
            du0[...] = du[:rows, :]

        @pl.when(s > 0)
        def _():
            across_sum(s).wait_recv()
            theirs = pltpu.make_async_copy(partner_sums.at[s], dyb.at[pl.ds(rows, rows)], load.at[2])
            theirs.start()

            @pl.when(s == 1)
            def _():
                dyb[:rows, :] = jnp.zeros((rows, depth), BF16)

            @pl.when(s > 1)
            def _():
                for d in range(2):
                    ring_sum(s - 1, d).wait_recv()
                    pltpu.make_async_copy(sums.at[s - 1, d], dyb.at[pl.ds(d * half, half)], load.at[d]).start()
                for d in range(2):
                    ring_sum(s - 1, d).wait_send()
                    pltpu.make_async_copy(sums.at[s - 1, d], dyb.at[pl.ds(d * half, half)], load.at[d]).wait()

            theirs.wait()

            def add(j, carry):
                cols = columns(j)
                total = term(dg[:rows, :], du[:rows, :], cols) + dyb[rows:, cols].astype(F32) + dyb[:rows, cols].astype(F32)
                to_ring[:, cols] = total.astype(BF16)
                return carry

            lax.fori_loop(0, tiles, add, 0)
            for d in range(2):
                ring_sum(s, d).start()

        gather_rest(xg, xb, s, x_sems, loadx)

        def gate_up(j, carry):
            cols = columns(j)
            acc_g[:, cols] += dot(dg_t[...], xb[:, cols])
            acc_u[:, cols] += dot(du_t[...], xb[:, cols])
            return carry

        lax.fori_loop(0, tiles, gate_up, 0)
        return carry

    lax.fori_loop(0, n, step, 0)

    across_sum(0).wait_recv()
    theirs = pltpu.make_async_copy(partner_sums.at[0], xb.at[pl.ds(0, rows)], load.at[2])
    theirs.start()

    def finish_down(j, carry):
        cols = columns(j)
        dyb[:, cols] = acc_d[:, cols].astype(BF16)
        return carry

    lax.fori_loop(0, tiles, finish_down, 0)
    out_d = pltpu.make_async_copy(dyb, dwd_out, load.at[3])
    out_d.start()
    theirs.wait()

    def own(j, carry):
        cols = columns(j)
        acc_d[:rows, cols] = term(dg0[...], du0[...], cols) + xb[:rows, cols].astype(F32)
        return carry

    lax.fori_loop(0, tiles, own, 0)

    def finish(acc, buf):
        def body(j, carry):
            cols = columns(j)
            buf[cols, :] = acc[:, cols].astype(BF16).T
            return carry

        lax.fori_loop(0, tiles, body, 0)

    finish(acc_g, wg)
    out_g = pltpu.make_async_copy(wg, dwg_out, load.at[4])
    out_g.start()
    finish(acc_u, wu)
    out_u = pltpu.make_async_copy(wu, dwu_out, load.at[5])
    out_u.start()

    last = []
    for d in range(2):
        ring_sum(n - 1, d).wait_recv()
        last.append(pltpu.make_async_copy(sums.at[n - 1, d], xb.at[pl.ds(rows + d * half, half)], load.at[d]))
        last[d].start()
    for d in range(2):
        ring_sum(n - 1, d).wait_send()
        last[d].wait()

    def finish_dx(j, carry):
        cols = columns(j)
        to_ring[:, cols] = (acc_d[:rows, cols] + xb[rows:, cols].astype(F32)).astype(BF16)
        return carry

    lax.fori_loop(0, tiles, finish_dx, 0)
    out_x = pltpu.make_async_copy(to_ring, dx_out, load.at[2])
    out_x.start()

    across_sum(n - 1).wait_send()

    def drain(s, carry):
        for mine, whole, sems in ((dy_in, dyg, dy_sems), (x_in, xg, x_sems)):
            for d in range(2):
                src = mine.at[pl.ds(d * half, half)]
                across(src, whole, s, d, sems).wait_send()

                @pl.when(s < n - 1)
                def _():
                    forward(src, whole, s, d, sems).wait_send()

        return carry

    lax.fori_loop(0, n, drain, 0)
    for copy in (out_d, out_g, out_u, out_x):
        copy.wait()


def solution(mesh):
    side = math.isqrt(mesh.shape["tp"] // 2)
    n = side * side
    assert 2 * n == mesh.shape["tp"]

    def step(x, dy, gate, up, w_gate, w_up, w_down):
        rows, depth = x.shape
        tokens, ff = gate.shape
        tile = min(512, depth)
        shape = jax.ShapeDtypeStruct
        any_space = pl.BlockSpec(memory_space=pl.ANY)
        dma = pltpu.SemaphoreType.DMA
        vmem = pltpu.VMEM
        outs = pl.pallas_call(
            functools.partial(kernel, side, tile),
            out_shape=[
                shape((rows, depth), BF16),
                shape((depth, ff), BF16),
                shape((depth, ff), BF16),
                shape((ff, depth), BF16),
                shape((tokens, depth), BF16),
                shape((tokens, depth), BF16),
                shape((n, 2, rows // 2, depth), BF16),
                shape((n, rows, depth), BF16),
            ],
            in_specs=[any_space] * 7,
            out_specs=[any_space] * 8,
            scratch_shapes=[
                vmem((depth, ff), BF16),
                vmem((depth, ff), BF16),
                vmem((ff, depth), BF16),
                vmem((ff, depth), F32),
                vmem((ff, depth), F32),
                vmem((ff, depth), F32),
                vmem((2 * rows, depth), BF16),
                vmem((2 * rows, depth), BF16),
                vmem((2 * rows, ff), BF16),
                vmem((2 * rows, ff), BF16),
                vmem((2 * rows, ff), BF16),
                vmem((2 * rows, ff), BF16),
                vmem((ff, 2 * rows), BF16),
                vmem((ff, 2 * rows), BF16),
                vmem((ff, 2 * rows), BF16),
                vmem((rows, ff), BF16),
                vmem((rows, ff), BF16),
                vmem((rows, depth), BF16),
                vmem((rows, depth), BF16),
                dma((12,)),
                dma((3,)),
                dma((4,)),
            ]
            + [dma((2, n)), dma((2, n + 1)), dma((2, n)), dma((2, n))] * 2
            + [dma((2, n)), dma((2, n)), dma((n,)), dma((n,))],
            compiler_params=pltpu.CompilerParams(
                collective_id=0, has_side_effects=True, vmem_limit_bytes=67_043_328
            ),
        )(x, dy, gate, up, w_gate, w_up, w_down)
        return tuple(outs[:4])

    tokens_spec = P(("dp", "tp"), None)
    return jax.shard_map(
        step,
        mesh=mesh,
        in_specs=(tokens_spec, tokens_spec, P("dp", "tp"), P("dp", "tp"), P(None, "tp"), P(None, "tp"), P("tp", None)),
        out_specs=(tokens_spec, P("dp", "tp"), P("dp", "tp"), tokens_spec),
        check_vma=False,
    )
```

time: 708 us -> 551 us (0.78)
  Pallas kernels: 0 us -> 536 us
  waiting for transfers between devices: 373 us -> 0 us
  matrix products: 301 us -> 0 us
  between operations: 14 us -> 0.65 us
    pallas_call x0 -> x1, Pallas kernels: none -> 536 us  [step(): pl.pallas_call(functools.partial(kernel, side, tile), out_shape=[shape((r...]
    unnamed x6 -> x0, waiting for transfers between devices: 373 us -> none
    dot_general x6 -> x0, matrix products: 301 us -> none  [the longest x3 142 us: by_group(): jnp.einsum('gta,gtb->gab', a, b, preferred_element_type=jnp.float32)]
  transfers between devices with their start and end apart: 3 -> 0, of which waited for: 3 -> 0; matrix products, arithmetic and copies ran while one was open for 45% -> 0% of each run, Pallas kernels for 0% -> 0%
where the time goes in v1:
time: 551 us; the launch traced here: 549 us
  Pallas kernels  536 us (97%)
  local copies, waits for them, and re-layouts  12.7 us (2%)
    pallas_call x1, Pallas kernels, step(): pl.pallas_call(functools.partial(kernel, side, tile), out_shape=[shape((r...  536 us
    unnamed x10, local copies, waits for them, and re-layouts  12.7 us

profile of v1, /device:TPU:97, one launch (start us, length us, event | category | flops | bytes accessed | tf_op | source)
XLA Modules:
  0.0 549.1 jit_solution(2037910237885142238)
XLA Ops:
  0.6 535.7 %shard_map.102 = (bf16[256,4096]{1,0:T(8,128)(2,1)}, bf16[4096,512]{1,0:T(8,128)(2,1)}, bf16[4096,512]{1,0:T(8,128)(2,1)}, bf16[512,4096]{1,0:T(8,128)(2,1)}, bf...) custom-call(bf16[256,4096]{1,0:T(8,128)(2,1)} %x_in.1, ...), custom_call_target="tpu_custom_call" | custom-call | tf_op jit(solution)/shard_map/pallas_call | solution.py:349
  536.4 0.0 copy-start.2
  536.4 3.3 copy.15
  539.7 0.0 copy-done.2
  539.7 0.0 copy-start.1
  539.7 2.1 copy.16
  541.8 1.6 copy-done.1
  543.4 0.0 copy-start
  543.4 2.1 copy.17
  545.5 1.6 copy-done
  547.1 2.0 copy.18
Async XLA Ops:
  536.4 3.3 copy-start.2
  539.7 3.7 copy-start.1
  543.4 3.7 copy-start

commit v2 on v1

--- a/solution.py
+++ b/solution.py
@@ -25,14 +25,15 @@
 def kernel(
     side, tile,
     x_in, dy_in, gate, up, w_gate, w_up, w_down,
-    dx_out, dwg_out, dwu_out, dwd_out, xg, dyg, sums, partner_sums,
-    wg, wu, wd, acc_g, acc_u, acc_d, dyb, xb, gb, ub, dg, du, hid_t, dg_t, du_t, dg0, du0, to_partner, to_ring,
+    to_ring, wg, wu, dyb, xg, dyg, sums, partner_sums,
+    wd, acc_g, acc_u, acc_d, xb, gb, ub, dg, du, hid_t, dg_t, du_t, to_partner, terms,
     load, loadw, loadx,
     dy_s, dy_r, dy_ps, dy_pr, x_s, x_r, x_ps, x_pr, rs_s, rs_r, ps_s, ps_r,
 ):
     n = side * side
     rows, depth = x_in.shape
     half = rows // 2
+    quarter = half // 2
     ff = gate.shape[1]
     tiles = depth // tile
 
@@ -124,9 +125,32 @@
     def across_sum(s):
         return remote(to_partner, partner_sums.at[s], ps_s.at[s], ps_r.at[s], partner)
 
-    def ring_sum(s, d):
-        src = to_ring.at[pl.ds(d * half, half)]
-        return remote(src, sums.at[s, d], rs_s.at[d, s], rs_r.at[d, s], onward[d])
+    def ring_sum(s, d, h):
+        src = to_ring.at[pl.ds(d * half + h * quarter, quarter)]
+        return remote(src, sums.at[s, d, h], rs_s.at[2 * d + h, s], rs_r.at[2 * d + h, s], onward[d])
+
+    def add_arrived(s, term_slot, buf, send):
+        def incoming(d, h):
+            at = pl.ds(d * half + h * quarter, quarter)
+            return pltpu.make_async_copy(sums.at[s, d, h], buf.at[at], load.at[d])
+
+        for h in range(2):
+            for d in range(2):
+                ring_sum(s, d, h).wait_recv()
+                incoming(d, h).start()
+            for d in range(2):
+                ring_sum(s, d, h).wait_send()
+                incoming(d, h).wait()
+                at = pl.ds(d * half + h * quarter, quarter)
+
+                def add(j, carry):
+                    cols = columns(j)
+                    to_ring[at, cols] = (terms[term_slot, at, cols] + buf[at, cols].astype(F32)).astype(BF16)
+                    return carry
+
+                lax.fori_loop(0, tiles, add, 0)
+                if send:
+                    ring_sum(s + 1, d, h).start()
 
     def term(a_gate, a_up, cols):
         return dot_t(a_gate, wg[cols, :]) + dot_t(a_up, wu[cols, :])
@@ -145,9 +169,12 @@
             at = pl.ds(piece(s, i), half)
             kept.append(pltpu.make_async_copy(gate.at[at], gb.at[pl.ds(i * half, half)], load.at[4 + i]))
             kept.append(pltpu.make_async_copy(up.at[at], ub.at[pl.ds(i * half, half)], load.at[8 + i]))
-        gather_step(dy_in, dyg, dyb, s, dy_sems, load)
         for copy in kept:
             copy.start()
+
+        @pl.when(s != 1)
+        def _():
+            gather_step(dy_in, dyg, dyb, s, dy_sems, load)
 
         @pl.when(s == 0)
         def _():
@@ -211,42 +238,9 @@
 
         lax.fori_loop(0, tiles, down, 0)
 
-        @pl.when(s == 0)
-        def _():
-            dg0[...] = dg[:rows, :]
-            du0[...] = du[:rows, :]
-
-        @pl.when(s > 0)
-        def _():
-            across_sum(s).wait_recv()
-            theirs = pltpu.make_async_copy(partner_sums.at[s], dyb.at[pl.ds(rows, rows)], load.at[2])
-            theirs.start()
-
-            @pl.when(s == 1)
-            def _():
-                dyb[:rows, :] = jnp.zeros((rows, depth), BF16)
-
-            @pl.when(s > 1)
-            def _():
-                for d in range(2):
-                    ring_sum(s - 1, d).wait_recv()
-                    pltpu.make_async_copy(sums.at[s - 1, d], dyb.at[pl.ds(d * half, half)], load.at[d]).start()
-                for d in range(2):
-                    ring_sum(s - 1, d).wait_send()
-                    pltpu.make_async_copy(sums.at[s - 1, d], dyb.at[pl.ds(d * half, half)], load.at[d]).wait()
-
-            theirs.wait()
-
-            def add(j, carry):
-                cols = columns(j)
-                total = term(dg[:rows, :], du[:rows, :], cols) + dyb[rows:, cols].astype(F32) + dyb[:rows, cols].astype(F32)
-                to_ring[:, cols] = total.astype(BF16)
-                return carry
-
-            lax.fori_loop(0, tiles, add, 0)
-            for d in range(2):
-                ring_sum(s, d).start()
-
+        across_sum(s).wait_recv()
+        theirs = pltpu.make_async_copy(partner_sums.at[s], dyb.at[pl.ds(rows, rows)], load.at[12])
+        theirs.start()
         gather_rest(xg, xb, s, x_sems, loadx)
 
         def gate_up(j, carry):
@@ -256,64 +250,49 @@
             return carry
 
         lax.fori_loop(0, tiles, gate_up, 0)
+
+        slot = lax.div(s + n - 1, n)
+        theirs.wait()
+
+        def own(j, carry):
+            cols = columns(j)
+            terms[slot, :, cols] = term(dg[:rows, :], du[:rows, :], cols) + dyb[rows:, cols].astype(F32)
+            return carry
+
+        lax.fori_loop(0, tiles, own, 0)
+
+        @pl.when(s == 0)
+        def _():
+            gather_step(dy_in, dyg, dyb, s + 1, dy_sems, load)
+
+        @pl.when(s == 1)
+        def _():
+            def first(j, carry):
+                cols = columns(j)
+                to_ring[:, cols] = terms[1, :, cols].astype(BF16)
+                return carry
+
+            lax.fori_loop(0, tiles, first, 0)
+            for h in range(2):
+                for d in range(2):
+                    ring_sum(s, d, h).start()
+
+        @pl.when(s > 1)
+        def _():
+            add_arrived(s - 1, 1, dyb, True)
+
         return carry
 
     lax.fori_loop(0, n, step, 0)
-
-    across_sum(0).wait_recv()
-    theirs = pltpu.make_async_copy(partner_sums.at[0], xb.at[pl.ds(0, rows)], load.at[2])
-    theirs.start()
 
     def finish_down(j, carry):
         cols = columns(j)
         dyb[:, cols] = acc_d[:, cols].astype(BF16)
+        wg[cols, :] = acc_g[:, cols].astype(BF16).T
+        wu[cols, :] = acc_u[:, cols].astype(BF16).T
         return carry
 
     lax.fori_loop(0, tiles, finish_down, 0)
-    out_d = pltpu.make_async_copy(dyb, dwd_out, load.at[3])
-    out_d.start()
-    theirs.wait()
-
-    def own(j, carry):
-        cols = columns(j)
-        acc_d[:rows, cols] = term(dg0[...], du0[...], cols) + xb[:rows, cols].astype(F32)
-        return carry
-
-    lax.fori_loop(0, tiles, own, 0)
-
-    def finish(acc, buf):
-        def body(j, carry):
-            cols = columns(j)
-            buf[cols, :] = acc[:, cols].astype(BF16).T
-            return carry
-
-        lax.fori_loop(0, tiles, body, 0)
-
-    finish(acc_g, wg)
-    out_g = pltpu.make_async_copy(wg, dwg_out, load.at[4])
-    out_g.start()
-    finish(acc_u, wu)
-    out_u = pltpu.make_async_copy(wu, dwu_out, load.at[5])
-    out_u.start()
-
-    last = []
-    for d in range(2):
-        ring_sum(n - 1, d).wait_recv()
-        last.append(pltpu.make_async_copy(sums.at[n - 1, d], xb.at[pl.ds(rows + d * half, half)], load.at[d]))
-        last[d].start()
-    for d in range(2):
-        ring_sum(n - 1, d).wait_send()
-        last[d].wait()
-
-    def finish_dx(j, carry):
-        cols = columns(j)
-        to_ring[:, cols] = (acc_d[:rows, cols] + xb[rows:, cols].astype(F32)).astype(BF16)
-        return carry
-
-    lax.fori_loop(0, tiles, finish_dx, 0)
-    out_x = pltpu.make_async_copy(to_ring, dx_out, load.at[2])
-    out_x.start()
-
     across_sum(n - 1).wait_send()
 
     def drain(s, carry):
@@ -329,8 +308,7 @@
         return carry
 
     lax.fori_loop(0, n, drain, 0)
-    for copy in (out_d, out_g, out_u, out_x):
-        copy.wait()
+    add_arrived(n - 1, 0, xb, False)
 
 
 def solution(mesh):
@@ -349,25 +327,22 @@
         outs = pl.pallas_call(
             functools.partial(kernel, side, tile),
             out_shape=[
-                shape((rows, depth), BF16),
-                shape((depth, ff), BF16),
-                shape((depth, ff), BF16),
-                shape((ff, depth), BF16),
+                pltpu.VMEM((rows, depth), BF16),
+                pltpu.VMEM((depth, ff), BF16),
+                pltpu.VMEM((depth, ff), BF16),
+                pltpu.VMEM((ff, depth), BF16),
                 shape((tokens, depth), BF16),
                 shape((tokens, depth), BF16),
-                shape((n, 2, rows // 2, depth), BF16),
+                shape((n, 2, 2, rows // 4, depth), BF16),
                 shape((n, rows, depth), BF16),
             ],
             in_specs=[any_space] * 7,
-            out_specs=[any_space] * 8,
+            out_specs=[pl.BlockSpec(memory_space=pltpu.VMEM)] * 4 + [any_space] * 4,
             scratch_shapes=[
-                vmem((depth, ff), BF16),
-                vmem((depth, ff), BF16),
                 vmem((ff, depth), BF16),
                 vmem((ff, depth), F32),
                 vmem((ff, depth), F32),
                 vmem((ff, depth), F32),
-                vmem((2 * rows, depth), BF16),
                 vmem((2 * rows, depth), BF16),
                 vmem((2 * rows, ff), BF16),
                 vmem((2 * rows, ff), BF16),
@@ -376,18 +351,16 @@
                 vmem((ff, 2 * rows), BF16),
                 vmem((ff, 2 * rows), BF16),
                 vmem((ff, 2 * rows), BF16),
-                vmem((rows, ff), BF16),
-                vmem((rows, ff), BF16),
                 vmem((rows, depth), BF16),
-                vmem((rows, depth), BF16),
-                dma((12,)),
+                vmem((2, rows, depth), F32),
+                dma((13,)),
                 dma((3,)),
                 dma((4,)),
             ]
             + [dma((2, n)), dma((2, n + 1)), dma((2, n)), dma((2, n))] * 2
-            + [dma((2, n)), dma((2, n)), dma((n,)), dma((n,))],
+            + [dma((4, n)), dma((4, n)), dma((n,)), dma((n,))],
             compiler_params=pltpu.CompilerParams(
-                collective_id=0, has_side_effects=True, vmem_limit_bytes=67_043_328
+                collective_id=0, has_side_effects=True, vmem_limit_bytes=48 * 2**20
             ),
         )(x, dy, gate, up, w_gate, w_up, w_down)
         return tuple(outs[:4])

time: 551 us -> 554 us (level)
  Pallas kernels: 536 us -> 544 us
    pallas_call x1, Pallas kernels: 536 us -> 544 us  [step(): pl.pallas_call(functools.partial(kernel, side, tile), out_shape=[pltpu.VM...]
    unnamed x10 -> x4, local copies, waits for them, and re-layouts: 12.7 us -> 7.36 us
where the time goes in v2:
time: 554 us; the launch traced here: 552 us
  Pallas kernels  544 us (98%)
  local copies, waits for them, and re-layouts  7.36 us (1%)
    pallas_call x1, Pallas kernels, step(): pl.pallas_call(functools.partial(kernel, side, tile), out_shape=[pltpu.VM...  544 us

profile of v2, /device:TPU:97, one launch (start us, length us, event | category | flops | bytes accessed | tf_op | source)
XLA Modules:
  0.0 552.2 jit_solution(7360045193877731276)
XLA Ops:
  0.6 544.2 %shard_map.102 = (bf16[256,4096]{1,0:T(8,128)(2,1)S(1)}, bf16[4096,512]{1,0:T(8,128)(2,1)S(1)}, bf16[4096,512]{1,0:T(8,128)(2,1)S(1)}, bf16[512,4096]{1,0:T(8,12...) custom-call(bf16[256,4096]{1,0:T(8,128)(2,1)} %x_in.1, ...), custom_call_target="tpu_custom_call" | custom-call | tf_op jit(solution)/shard_map/pallas_call | solution.py:327
  544.9 1.3 copy.15
  546.2 2.0 copy.16
  548.2 2.0 copy.17
  550.2 2.0 copy.18

commit v3 on v2

--- a/solution.py
+++ b/solution.py
@@ -129,28 +129,38 @@
         src = to_ring.at[pl.ds(d * half + h * quarter, quarter)]
         return remote(src, sums.at[s, d, h], rs_s.at[2 * d + h, s], rs_r.at[2 * d + h, s], onward[d])
 
+    def theirs_load(s, buf):
+        return pltpu.make_async_copy(partner_sums.at[s], buf.at[pl.ds(rows, rows)], load.at[12])
+
     def add_arrived(s, term_slot, buf, send):
         def incoming(d, h):
             at = pl.ds(d * half + h * quarter, quarter)
-            return pltpu.make_async_copy(sums.at[s, d, h], buf.at[at], load.at[d])
+            return pltpu.make_async_copy(sums.at[last(s), d, h], buf.at[at], load.at[d])
+
+        def last(s):
+            return s - 1 if send else n - 1
 
         for h in range(2):
             for d in range(2):
-                ring_sum(s, d, h).wait_recv()
+                ring_sum(last(s), d, h).wait_recv()
                 incoming(d, h).start()
+            if h == 0:
+                theirs_load(s, buf).wait()
             for d in range(2):
-                ring_sum(s, d, h).wait_send()
+                ring_sum(last(s), d, h).wait_send()
                 incoming(d, h).wait()
                 at = pl.ds(d * half + h * quarter, quarter)
+                across_at = pl.ds(rows + d * half + h * quarter, quarter)
 
                 def add(j, carry):
                     cols = columns(j)
-                    to_ring[at, cols] = (terms[term_slot, at, cols] + buf[at, cols].astype(F32)).astype(BF16)
+                    total = terms[term_slot, at, cols] + buf[across_at, cols].astype(F32) + buf[at, cols].astype(F32)
+                    to_ring[at, cols] = total.astype(BF16)
                     return carry
 
                 lax.fori_loop(0, tiles, add, 0)
                 if send:
-                    ring_sum(s + 1, d, h).start()
+                    ring_sum(s, d, h).start()
 
     def term(a_gate, a_up, cols):
         return dot_t(a_gate, wg[cols, :]) + dot_t(a_up, wu[cols, :])
@@ -215,16 +225,20 @@
 
         lax.fori_loop(0, ff // ff_tile, activate, 0)
 
+        slot = lax.div(s + n - 1, n)
+
         @pl.when(s > 0)
         def _():
             across_sum(s - 1).wait_send()
 
-        def for_partner(j, carry):
+        def own_terms(j, carry):
             cols = columns(j)
-            to_partner[:, cols] = term(dg[rows:, :], du[rows:, :], cols).astype(BF16)
+            both = term(dg[...], du[...], cols)
+            to_partner[:, cols] = both[rows:].astype(BF16)
+            terms[slot, :, cols] = both[:rows]
             return carry
 
-        lax.fori_loop(0, tiles, for_partner, 0)
+        lax.fori_loop(0, tiles, own_terms, 0)
         across_sum(s).start()
 
         @pl.when(s > 0)
@@ -238,9 +252,32 @@
 
         lax.fori_loop(0, tiles, down, 0)
 
-        across_sum(s).wait_recv()
-        theirs = pltpu.make_async_copy(partner_sums.at[s], dyb.at[pl.ds(rows, rows)], load.at[12])
-        theirs.start()
+        @pl.when(s == 0)
+        def _():
+            gather_step(dy_in, dyg, dyb, s + 1, dy_sems, load)
+
+        @pl.when(s == 1)
+        def _():
+            across_sum(s).wait_recv()
+            theirs_load(s, dyb).start()
+            theirs_load(s, dyb).wait()
+
+            def first(j, carry):
+                cols = columns(j)
+                to_ring[:, cols] = (terms[1, :, cols] + dyb[rows:, cols].astype(F32)).astype(BF16)
+                return carry
+
+            lax.fori_loop(0, tiles, first, 0)
+            for h in range(2):
+                for d in range(2):
+                    ring_sum(s, d, h).start()
+
+        @pl.when(s > 1)
+        def _():
+            across_sum(s).wait_recv()
+            theirs_load(s, dyb).start()
+            add_arrived(s, 1, dyb, True)
+
         gather_rest(xg, xb, s, x_sems, loadx)
 
         def gate_up(j, carry):
@@ -251,39 +288,12 @@
 
         lax.fori_loop(0, tiles, gate_up, 0)
 
-        slot = lax.div(s + n - 1, n)
-        theirs.wait()
-
-        def own(j, carry):
-            cols = columns(j)
-            terms[slot, :, cols] = term(dg[:rows, :], du[:rows, :], cols) + dyb[rows:, cols].astype(F32)
-            return carry
-
-        lax.fori_loop(0, tiles, own, 0)
-
-        @pl.when(s == 0)
-        def _():
-            gather_step(dy_in, dyg, dyb, s + 1, dy_sems, load)
-
-        @pl.when(s == 1)
-        def _():
-            def first(j, carry):
-                cols = columns(j)
-                to_ring[:, cols] = terms[1, :, cols].astype(BF16)
-                return carry
-
-            lax.fori_loop(0, tiles, first, 0)
-            for h in range(2):
-                for d in range(2):
-                    ring_sum(s, d, h).start()
-
-        @pl.when(s > 1)
-        def _():
-            add_arrived(s - 1, 1, dyb, True)
-
         return carry
 
     lax.fori_loop(0, n, step, 0)
+
+    across_sum(0).wait_recv()
+    theirs_load(0, xb).start()
 
     def finish_down(j, carry):
         cols = columns(j)
@@ -308,7 +318,7 @@
         return carry
 
     lax.fori_loop(0, n, drain, 0)
-    add_arrived(n - 1, 0, xb, False)
+    add_arrived(0, 0, xb, False)
 
 
 def solution(mesh):

time: 554 us -> 538 us (0.971)
  Pallas kernels: 544 us -> 528 us
    pallas_call x1, Pallas kernels: 544 us -> 528 us  [step(): pl.pallas_call(functools.partial(kernel, side, tile), out_shape=[pltpu.VM...]
where the time goes in v3:
time: 538 us; the launch traced here: 536 us
  Pallas kernels  528 us (98%)
  local copies, waits for them, and re-layouts  7.36 us (1%)
    pallas_call x1, Pallas kernels, step(): pl.pallas_call(functools.partial(kernel, side, tile), out_shape=[pltpu.VM...  528 us

profile of v3, /device:TPU:97, one launch (start us, length us, event | category | flops | bytes accessed | tf_op | source)
XLA Modules:
  0.0 535.7 jit_solution(13204219234680313742)
XLA Ops:
  0.6 527.7 %shard_map.102 = (bf16[256,4096]{1,0:T(8,128)(2,1)S(1)}, bf16[4096,512]{1,0:T(8,128)(2,1)S(1)}, bf16[4096,512]{1,0:T(8,128)(2,1)S(1)}, bf16[512,4096]{1,0:T(8,12...) custom-call(bf16[256,4096]{1,0:T(8,128)(2,1)} %x_in.1, ...), custom_call_target="tpu_custom_call" | custom-call | tf_op jit(solution)/shard_map/pallas_call | solution.py:337
  528.3 1.3 copy.15
  529.6 2.0 copy.16
  531.7 2.0 copy.17
  533.7 2.0 copy.18

commit v4 on v3

--- a/solution.py
+++ b/solution.py
@@ -26,7 +26,7 @@
     side, tile,
     x_in, dy_in, gate, up, w_gate, w_up, w_down,
     to_ring, wg, wu, dyb, xg, dyg, sums, partner_sums,
-    wd, acc_g, acc_u, acc_d, xb, gb, ub, dg, du, hid_t, dg_t, du_t, to_partner, terms,
+    wd, acc_g, acc_u, acc_d, xb, gb, ub, dg, du, hid_t, dg_t, du_t, to_partner, terms, landed,
     load, loadw, loadx,
     dy_s, dy_r, dy_ps, dy_pr, x_s, x_r, x_ps, x_pr, rs_s, rs_r, ps_s, ps_r,
 ):
@@ -129,38 +129,48 @@
         src = to_ring.at[pl.ds(d * half + h * quarter, quarter)]
         return remote(src, sums.at[s, d, h], rs_s.at[2 * d + h, s], rs_r.at[2 * d + h, s], onward[d])
 
+    def last_sum(d, h):
+        at = pl.ds(d * half + h * quarter, quarter)
+        return remote(to_ring.at[at], landed.at[at], rs_s.at[2 * d + h, n - 1], rs_r.at[2 * d + h, n - 1], onward[d])
+
     def theirs_load(s, buf):
         return pltpu.make_async_copy(partner_sums.at[s], buf.at[pl.ds(rows, rows)], load.at[12])
 
-    def add_arrived(s, term_slot, buf, send):
+    def sum_up(slot, d, h, arrived, theirs):
+        at = pl.ds(d * half + h * quarter, quarter)
+        theirs_at = pl.ds(rows + d * half + h * quarter, quarter)
+
+        def add(j, carry):
+            cols = columns(j)
+            total = terms[slot, at, cols] + theirs[theirs_at, cols].astype(F32) + arrived[at, cols].astype(F32)
+            to_ring[at, cols] = total.astype(BF16)
+            return carry
+
+        lax.fori_loop(0, tiles, add, 0)
+
+    def add_arrived(s):
         def incoming(d, h):
             at = pl.ds(d * half + h * quarter, quarter)
-            return pltpu.make_async_copy(sums.at[last(s), d, h], buf.at[at], load.at[d])
-
-        def last(s):
-            return s - 1 if send else n - 1
+            return pltpu.make_async_copy(sums.at[s - 1, d, h], dyb.at[at], load.at[d])
 
         for h in range(2):
             for d in range(2):
-                ring_sum(last(s), d, h).wait_recv()
+                ring_sum(s - 1, d, h).wait_recv()
                 incoming(d, h).start()
             if h == 0:
-                theirs_load(s, buf).wait()
+                theirs_load(s, dyb).wait()
             for d in range(2):
-                ring_sum(last(s), d, h).wait_send()
+                ring_sum(s - 1, d, h).wait_send()
                 incoming(d, h).wait()
-                at = pl.ds(d * half + h * quarter, quarter)
-                across_at = pl.ds(rows + d * half + h * quarter, quarter)
-
-                def add(j, carry):
-                    cols = columns(j)
-                    total = terms[term_slot, at, cols] + buf[across_at, cols].astype(F32) + buf[at, cols].astype(F32)
-                    to_ring[at, cols] = total.astype(BF16)
-                    return carry
-
-                lax.fori_loop(0, tiles, add, 0)
-                if send:
+                sum_up(1, d, h, dyb, dyb)
+
+                @pl.when(s < n - 1)
+                def _():
                     ring_sum(s, d, h).start()
+
+                @pl.when(s == n - 1)
+                def _():
+                    last_sum(d, h).start()
 
     def term(a_gate, a_up, cols):
         return dot_t(a_gate, wg[cols, :]) + dot_t(a_up, wu[cols, :])
@@ -225,6 +235,10 @@
 
         lax.fori_loop(0, ff // ff_tile, activate, 0)
 
+        @pl.when(s > 0)
+        def _():
+            gather_step(x_in, xg, xb, s, x_sems, loadx)
+
         slot = lax.div(s + n - 1, n)
 
         @pl.when(s > 0)
@@ -241,10 +255,6 @@
         lax.fori_loop(0, tiles, own_terms, 0)
         across_sum(s).start()
 
-        @pl.when(s > 0)
-        def _():
-            gather_step(x_in, xg, xb, s, x_sems, loadx)
-
         def down(j, carry):
             cols = columns(j)
             acc_d[:, cols] += dot(hid_t[...], dyb[:, cols])
@@ -276,7 +286,7 @@
         def _():
             across_sum(s).wait_recv()
             theirs_load(s, dyb).start()
-            add_arrived(s, 1, dyb, True)
+            add_arrived(s)
 
         gather_rest(xg, xb, s, x_sems, loadx)
 
@@ -318,7 +328,20 @@
         return carry
 
     lax.fori_loop(0, n, drain, 0)
-    add_arrived(0, 0, xb, False)
+    theirs_load(0, xb).wait()
+    for h in range(2):
+        for d in range(2):
+            last_sum(d, h).wait()
+            sum_up(0, d, h, landed, xb)
+
+
+def store(*refs):
+    held, out, sem = refs[:4], refs[4:8], refs[8]
+    copies = [pltpu.make_async_copy(a, b, sem.at[i]) for i, (a, b) in enumerate(zip(held, out))]
+    for copy in copies:
+        copy.start()
+    for copy in copies:
+        copy.wait()
 
 
 def solution(mesh):
@@ -363,6 +386,7 @@
                 vmem((ff, 2 * rows), BF16),
                 vmem((rows, depth), BF16),
                 vmem((2, rows, depth), F32),
+                vmem((rows, depth), BF16),
                 dma((13,)),
                 dma((3,)),
                 dma((4,)),
@@ -370,10 +394,17 @@
             + [dma((2, n)), dma((2, n + 1)), dma((2, n)), dma((2, n))] * 2
             + [dma((4, n)), dma((4, n)), dma((n,)), dma((n,))],
             compiler_params=pltpu.CompilerParams(
-                collective_id=0, has_side_effects=True, vmem_limit_bytes=48 * 2**20
+                collective_id=0, has_side_effects=True, vmem_limit_bytes=199 * 2**18
             ),
         )(x, dy, gate, up, w_gate, w_up, w_down)
-        return tuple(outs[:4])
+        return pl.pallas_call(
+            store,
+            out_shape=[shape(out.shape, BF16) for out in outs[:4]],
+            in_specs=[pl.BlockSpec(memory_space=vmem)] * 4,
+            out_specs=[any_space] * 4,
+            scratch_shapes=[dma((4,))],
+            compiler_params=pltpu.CompilerParams(vmem_limit_bytes=2**20),
+        )(*[pltpu.with_memory_space_constraint(out, vmem) for out in outs[:4]])
 
     tokens_spec = P(("dp", "tp"), None)
     return jax.shard_map(

time: 538 us -> 530 us (0.985)
  local copies, waits for them, and re-layouts: 7.36 us -> 0 us
    unnamed x4 -> x0, local copies, waits for them, and re-layouts: 7.36 us -> none
    pallas_call x0 -> x1, Pallas kernels: none -> 5.38 us  [step(): pl.pallas_call(store, out_shape=[shape(out.shape, BF16) for out in outs[:...]
where the time goes in v4:
time: 530 us; the launch traced here: 529 us
  Pallas kernels  528 us (100%)
    pallas_call x1, Pallas kernels, step(): pl.pallas_call(functools.partial(kernel, side, tile), out_shape=[pltpu.VM...  523 us

profile of v4, /device:TPU:97, one launch (start us, length us, event | category | flops | bytes accessed | tf_op | source)
XLA Modules:
  0.0 528.6 jit_solution(13031106480082751101)
XLA Ops:
  0.6 522.5 %shard_map.102 = (bf16[256,4096]{1,0:T(8,128)(2,1)S(1)}, bf16[4096,512]{1,0:T(8,128)(2,1)S(1)}, bf16[4096,512]{1,0:T(8,128)(2,1)S(1)}, bf16[512,4096]{1,0:T(8,12...) custom-call(bf16[256,4096]{1,0:T(8,128)(2,1)} %x_in.1, ...), custom_call_target="tpu_custom_call" | custom-call | tf_op jit(solution)/shard_map/pallas_call | solution.py:360
  523.2 5.4 %shard_map.103 = (bf16[256,4096]{1,0:T(8,128)(2,1)}, bf16[4096,512]{1,0:T(8,128)(2,1)}, bf16[4096,512]{1,0:T(8,128)(2,1)}, bf16[512,4096]{1,0:T(8,128)(2,1)}) custom-call(bf16[256,4096]{1,0:T(8,128)(2,1)S(1)} %get-tuple-element.8.refs_0_, bf16[4096,512]{1,0:T(8,128)(2,1)S(1)} %get-tuple-element.9.refs_1_, bf16[4096,512]{1,0:T(8,128)(2,1)S(1)} %get-tuple-element.10.refs_2_, ...), custom_call_target="tpu_custom_call" | custom-call | tf_op jit(solution)/shard_map/pallas_call | solution.py:400
